TPU v7x, 32 devices: a whole 2x2x4 slice. The times are simulated.
32 devices in a mesh: dp: 8 (over y, x, core), expert: 4 (over z).
Axes of the slice: x: 2, y: 2, z: 4, core: 2. Of those that a mesh axis runs over, the one named last changes fastest.
Arguments:
- out_grad: bfloat16 [64, 4096], P(('dp', 'expert')), may hold values from -0.29882812 to 0.29882812
- routes: int32 [64, 2], P('dp'), may hold values from 0 to 7, all different within a row; in each aligned block of 8 rows (0 to 7, 8 to 15, ...) at most 3 rows name the same one
- gate_values: bfloat16 [64, 2], P(('dp', 'expert')), may hold values from 0.099609375 to 1
- gate_pre: bfloat16 [8, 24, 12288], P('expert', None, 'dp'), may hold values from -6 to 6
- up_pre: bfloat16 [8, 24, 12288], P('expert', None, 'dp'), may hold values from -6 to 6
- w_down: bfloat16 [8, 12288, 4096], P('expert', 'dp'), may hold values from -0.0546875 to 0.0546875
Outputs:
- grad_gates: float32 [64, 2], P(('dp', 'expert'))
- grad_gate_pre: bfloat16 [8, 24, 12288], P('expert', None, 'dp')
- grad_up_pre: bfloat16 [8, 24, 12288], P('expert', None, 'dp')
- grad_down: bfloat16 [8, 12288, 4096], P('expert', 'dp')
Inputs may be any that keep to these rules, and one draw needn't show every extreme that they name: `routes`: each token names two different experts. Among the 8 tokens of one block (aligned blocks of tokens, one for each dp index) no expert is named more than 3 times, and some expert reaches 3 in some block.
All inputs are finite; a program needn't handle non-finite values.
Results may differ from a plain program's by a relative error of at most 0.0049.
Values may be sent and summed in bfloat16 or wider, within the bound.
A program may use at most 128 MiB of HBM per device.

v0:
```python
import functools

import jax
import jax.numpy as jnp
from jax import lax
from jax.experimental import pallas as pl
from jax.experimental.pallas import tpu as pltpu
from jax.sharding import PartitionSpec as P

SLOTS = 3


def expert_terms(gate_piece, up_piece, weights, rows_in, gate_row):
    projected = jnp.einsum("erd,efd->erf", rows_in, weights, preferred_element_type=jnp.float32)
    gate_act = gate_piece.astype(jnp.float32)
    up_act = up_piece.astype(jnp.float32)
    sigmoid_val = jax.nn.sigmoid(gate_act)
    silu_val = gate_act * sigmoid_val
    hidden = silu_val * up_act
    partial_value = jnp.sum(hidden * projected, axis=2)
    scale_col = gate_row.astype(jnp.float32)[:, :, None]
    weighted = (scale_col * hidden).astype(jnp.bfloat16)
    down_term = jnp.einsum("erf,erd->efd", weighted, rows_in, preferred_element_type=jnp.float32)
    grad_hidden = scale_col * projected
    grad_gate = (
        grad_hidden * up_act * sigmoid_val * (1.0 + gate_act * (1.0 - sigmoid_val))
    ).astype(jnp.bfloat16)
    grad_up = (grad_hidden * silu_val).astype(jnp.bfloat16)
    return (partial_value, grad_gate, grad_up, down_term)


def general_device(out_grad, routes, gate_values, gate_pre, up_pre, w_down):
    groups = lax.axis_size("expert")
    local_count = gate_pre.shape[0]
    experts = local_count * groups
    tok_count = out_grad.shape[0]
    my_rank = lax.axis_index("expert")
    flat_routes = routes.reshape(-1)
    onehot = (flat_routes[:, None] == jnp.arange(experts, dtype=jnp.int32)[None, :]).astype(
        jnp.int32
    )
    position = jnp.sum((jnp.cumsum(onehot, axis=0) - 1) * onehot, axis=1)
    own_expert = lax.dynamic_slice_in_dim(flat_routes, my_rank * tok_count * 2, tok_count * 2)
    own_position = lax.dynamic_slice_in_dim(position, my_rank * tok_count * 2, tok_count * 2)
    target = own_expert * SLOTS + own_position
    selector = target[:, None] == jnp.arange(experts * SLOTS, dtype=jnp.int32)[None, :]
    picker = selector.astype(jnp.bfloat16).T
    pair_rows = jnp.repeat(out_grad, 2, axis=0)
    send_rows = (
        jnp.dot(picker, pair_rows, preferred_element_type=jnp.float32)
        .astype(jnp.bfloat16)
        .reshape(experts, SLOTS, -1)
    )
    send_gates = (
        jnp.dot(picker, gate_values.reshape(-1, 1), preferred_element_type=jnp.float32)
        .astype(jnp.bfloat16)
        .reshape(experts, SLOTS)
    )
    got_rows, got_gates = (
        lax.all_to_all(send_rows, "expert", split_axis=0, concat_axis=0, tiled=True),
        lax.all_to_all(send_gates, "expert", split_axis=0, concat_axis=0, tiled=True),
    )
    dispatched = jnp.sum(
        got_rows.reshape(groups, local_count, SLOTS, -1).astype(jnp.float32), axis=0
    ).astype(jnp.bfloat16)
    slot_gate = jnp.sum(
        got_gates.reshape(groups, local_count, SLOTS).astype(jnp.float32), axis=0
    ).astype(jnp.bfloat16)
    all_rows, all_gates = (
        lax.all_gather(dispatched, "dp", axis=1, tiled=True),
        lax.all_gather(slot_gate, "dp", axis=1, tiled=True),
    )
    partial_value, grad_gate_pre, grad_up_pre, down_sum = expert_terms(
        gate_pre, up_pre, w_down, all_rows, all_gates
    )
    grad_down = down_sum.astype(jnp.bfloat16)
    own_sums = lax.psum_scatter(partial_value, "dp", scatter_dimension=1, tiled=True)
    score_table = lax.all_gather(own_sums, "expert", axis=0, tiled=True)
    picked = jnp.sum(jnp.where(selector, score_table.reshape(1, -1), 0.0), axis=1)
    grad_gates = picked.reshape(tok_count, 2)
    return (grad_gates, grad_gate_pre, grad_up_pre, grad_down)


LANES = 128
CORES = 2
MESH = pl.DeviceIdType.MESH


def pow2(n):
    return n & (n - 1) == 0


def fused_fits(n_dp, groups, tokens, width, local, rows, hidden):
    if 16 % tokens or n_dp % CORES:
        return False
    split = 16 // tokens
    padded = -(-rows // 16) * 16
    return (
        width % (split * LANES) == 0
        and hidden % 512 == 0
        and local * padded <= LANES
        and pow2(split)
        and pow2(groups)
        and n_dp * groups <= 64
        and rows == n_dp * SLOTS
        and local * hidden * width * 2 <= 32 << 20
    )


def gather_project(
    n_dp, groups, split, local, rows, padded, block,
    payload, gate_pre, up_pre, weights,
    rows_out, gates_out, proj_out, grads_out,
    table, held, sums_own, sums_all,
    load_sem, own_sem, send_z, recv_z, send_c, recv_c, send_p, recv_p, send_s, recv_s,
):
    me_dp, me_z = lax.axis_index("dp"), lax.axis_index("expert")
    total = n_dp * groups
    me = me_dp * groups + me_z
    chips = n_dp // CORES
    chip, core = me_dp // CORES, lax.rem(me_dp, CORES)
    hidden = held.shape[1]
    per = hidden // block
    chunk = payload.shape[1] - LANES

    loads = []
    for e in range(local):
        for b in range(per):
            copy = pltpu.make_async_copy(
                weights.at[e, pl.ds(b * block, block)],
                held.at[e, pl.ds(b * block, block)],
                load_sem.at[e * per + b],
            )
            copy.start()
            loads.append(copy)
    keep = pltpu.make_async_copy(payload, table.at[me], own_sem)
    keep.start()

    barrier = pltpu.get_barrier_semaphore()
    for off in range(1, total):
        other = lax.rem(me + off, total)
        pl.semaphore_signal(
            barrier, inc=1, device_id=(other // groups, lax.rem(other, groups)), device_id_type=MESH
        )
    pl.semaphore_wait(barrier, total - 1)

    sent = []
    first = []
    for dz in range(1, groups):
        copy = pltpu.make_async_remote_copy(
            src_ref=payload,
            dst_ref=table.at[me],
            send_sem=send_z.at[dz],
            recv_sem=recv_z.at[dz],
            device_id=(me_dp, lax.rem(me_z + dz, groups)),
            device_id_type=MESH,
        )
        copy.start()
        first.append(copy)
    sent += first
    keep.wait()
    for copy in first:
        copy.wait_recv()

    def block_copy(dp_index, target, s_sem, r_sem):
        copy = pltpu.make_async_remote_copy(
            src_ref=table.at[pl.ds(dp_index * groups, groups)],
            dst_ref=table.at[pl.ds(dp_index * groups, groups)],
            send_sem=s_sem,
            recv_sem=r_sem,
            device_id=(target, me_z),
            device_id_type=MESH,
        )
        copy.start()
        return copy

    second = []
    for dc in range(1, chips):
        target = lax.rem(chip + dc, chips) * CORES + core
        second.append(block_copy(me_dp, target, send_c.at[dc], recv_c.at[dc]))
    partner = chip * CORES + (1 - core)
    third = [block_copy(me_dp, partner, send_p.at[0], recv_p.at[0])]
    for dc in range(1, chips):
        second[dc - 1].wait_recv()
        source = lax.rem(chip - dc + chips, chips) * CORES + core
        third.append(block_copy(source, partner, send_p.at[dc], recv_p.at[dc]))
    for copy in third:
        copy.wait_recv()
    sent += second + third

    depth = total * 16
    wide = local * padded
    data = table[...].reshape(depth, chunk + LANES)
    meta_low = data[:, chunk:]
    meta = meta_low.astype(jnp.float32)
    row = lax.broadcasted_iota(jnp.int32, (depth, 1), 0)
    piece = (row & (split - 1)).astype(jnp.float32)
    col = lax.broadcasted_iota(jnp.int32, (depth, split * wide), 1).astype(jnp.float32)
    low = (me_z * local).astype(jnp.float32)
    picks = []
    for k in range(2):
        offset = meta[:, 2 * k : 2 * k + 1] - low
        code = piece * wide + offset * padded + meta[:, 2 * k + 1 : 2 * k + 2]
        code = jnp.where((offset >= 0) & (offset < local), code, -1.0)
        picks.append(jnp.where(col == code, 1.0, 0.0))
    either = (picks[0] + picks[1]).T.astype(jnp.bfloat16)
    slots = jnp.dot(either, data[:, :chunk], preferred_element_type=jnp.float32).astype(jnp.bfloat16)
    for c in range(split):
        for e in range(local):
            at = c * wide + e * padded
            rows_out[e, :, c * chunk : (c + 1) * chunk] = slots[at : at + padded]
    scale = jnp.zeros((wide, 1), jnp.float32)
    for k in range(2):
        pick = picks[k][:, :LANES].T.astype(jnp.bfloat16)
        got = jnp.dot(pick, meta_low, preferred_element_type=jnp.float32)
        scale = scale + got[:wide, 4 + k : 5 + k]
    for e in range(local):
        gates_out[e] = jnp.broadcast_to(scale[e * padded : (e + 1) * padded], (padded, LANES))

    lane = lax.broadcasted_iota(jnp.int32, (rows, LANES), 1)
    slot = lax.broadcasted_iota(jnp.int32, (rows, LANES), 0)
    mine = jnp.zeros((1, LANES), jnp.float32)
    for e in range(local):
        part = jnp.zeros((rows, 1), jnp.float32)
        for b in range(per):
            loads[e * per + b].wait()
            span = slice(b * block, (b + 1) * block)
            proj = lax.dot_general(
                rows_out[e], held[e, span], (((1,), (1,)), ((), ())),
                preferred_element_type=jnp.float32,
            )[:rows]
            proj_out[e, :, span] = proj
            gate_act = gate_pre[e, :, span].astype(jnp.float32)
            up_act = up_pre[e, :, span].astype(jnp.float32)
            silu_val = gate_act * jax.nn.sigmoid(gate_act)
            part = part + jnp.sum(silu_val * up_act * proj, axis=1, keepdims=True)
        mine = mine + jnp.sum(
            jnp.where(lane == slot + e * padded, part, 0.0), axis=0, keepdims=True
        )
    sums_own[...] = mine
    sums_all[me] = mine
    last = []
    for off in range(1, total):
        other = lax.rem(me + off, total)
        copy = pltpu.make_async_remote_copy(
            src_ref=sums_own,
            dst_ref=sums_all.at[me],
            send_sem=send_s.at[off],
            recv_sem=recv_s.at[off],
            device_id=(other // groups, lax.rem(other, groups)),
            device_id_type=MESH,
        )
        copy.start()
        last.append(copy)
    for copy in last:
        copy.wait_recv()
    sent += last

    own = payload[:, chunk:].astype(jnp.float32)
    lane_at = lax.broadcasted_iota(jnp.int32, (1, LANES), 1)
    out_row = lax.broadcasted_iota(jnp.int32, grads_out.shape, 0)
    out_col = lax.broadcasted_iota(jnp.int32, grads_out.shape, 1)
    by_group = []
    for z in range(groups):
        acc = sums_all[z]
        for d in range(1, n_dp):
            acc = acc + sums_all[d * groups + z]
        by_group.append(acc)
    result = jnp.zeros(grads_out.shape, jnp.float32)
    for t in range(16 // split):
        for k in range(2):
            expert = own[t * split : t * split + 1, 2 * k : 2 * k + 1]
            spot = own[t * split : t * split + 1, 2 * k + 1 : 2 * k + 2]
            value = jnp.zeros((1, LANES), jnp.float32)
            for z in range(groups):
                offset = expert - z * local
                code = jnp.where((offset >= 0) & (offset < local), offset * padded + spot, -1.0)
                value = value + jnp.where(lane_at.astype(jnp.float32) == code, by_group[z], 0.0)
            value = jnp.sum(value, axis=1, keepdims=True)
            result = jnp.where((out_row == t) & (out_col == k), value, result)
    grads_out[...] = result
    for copy in sent:
        copy.wait_send()


def finish(
    rows, proj, rows_in, gates, gate_pre, up_pre, sums, grad_gate, grad_up, grad_down, grad_sums
):
    grad_sums[...] = sums[...]
    gate_act = gate_pre[0].astype(jnp.float32)
    up_act = up_pre[0].astype(jnp.float32)
    sigmoid_val = jax.nn.sigmoid(gate_act)
    silu_val = gate_act * sigmoid_val
    scale = gates[0, :rows, 0:1]
    grad_hidden = scale * proj[0]
    grad_gate[0] = (
        grad_hidden * up_act * sigmoid_val * (1.0 + gate_act * (1.0 - sigmoid_val))
    ).astype(jnp.bfloat16)
    grad_up[0] = (grad_hidden * silu_val).astype(jnp.bfloat16)
    weighted = scale * (silu_val * up_act)
    fill = rows_in.shape[1] - rows
    if fill:
        weighted = jnp.concatenate(
            [weighted, jnp.zeros((fill, weighted.shape[1]), jnp.float32)], axis=0
        )
    turned = weighted.T.astype(jnp.bfloat16)
    step = 512
    for c in range(0, rows_in.shape[2], step):
        grad_down[0, :, c : c + step] = jnp.dot(
            turned, rows_in[0, :, c : c + step], preferred_element_type=jnp.float32
        ).astype(jnp.bfloat16)


def fused_device(out_grad, routes, gate_values, gate_pre, up_pre, w_down):
    n_dp, groups = lax.axis_size("dp"), lax.axis_size("expert")
    tokens, width = out_grad.shape
    local, rows, hidden = gate_pre.shape
    split = 16 // tokens
    chunk = width // split
    padded = -(-rows // 16) * 16
    block = 512
    total = n_dp * groups
    me_dp, me_z = lax.axis_index("dp"), lax.axis_index("expert")

    flat = routes.reshape(-1)
    count = flat.shape[0]
    earlier = jnp.arange(count)[None, :] < jnp.arange(count)[:, None]
    position = jnp.sum(((flat[:, None] == flat[None, :]) & earlier).astype(jnp.int32), axis=1)
    both = jnp.stack([flat, position + me_dp * SLOTS], axis=1).reshape(groups, tokens, 4)
    pick = (jnp.arange(groups) == me_z)[:, None, None]
    codes = jnp.sum(jnp.where(pick, both, 0), axis=0).astype(jnp.bfloat16)
    meta = jnp.concatenate([codes, gate_values], axis=1)
    meta = jnp.pad(meta, ((0, 0), (0, LANES - 6)))
    meta = jnp.broadcast_to(meta[:, None, :], (tokens, split, LANES)).reshape(16, LANES)
    payload = jnp.concatenate([out_grad.reshape(16, chunk), meta], axis=1)

    vmem = pl.BlockSpec(memory_space=pltpu.VMEM)
    dma = pltpu.SemaphoreType.DMA
    chips = n_dp // CORES
    rows_in, gates, proj, sums = pl.pallas_call(
        functools.partial(
            gather_project, n_dp, groups, split, local, rows, padded, block
        ),
        out_shape=(
            jax.ShapeDtypeStruct((local, padded, width), jnp.bfloat16),
            jax.ShapeDtypeStruct((local, padded, LANES), jnp.float32),
            jax.ShapeDtypeStruct((local, rows, hidden), jnp.float32),
            jax.ShapeDtypeStruct((tokens, 2), jnp.float32),
        ),
        in_specs=[vmem, vmem, vmem, pl.BlockSpec(memory_space=pl.ANY)],
        out_specs=(vmem, vmem, vmem, vmem),
        scratch_shapes=[
            pltpu.VMEM((total, 16, chunk + LANES), jnp.bfloat16),
            pltpu.VMEM((local, hidden, width), jnp.bfloat16),
            pltpu.VMEM((1, LANES), jnp.float32),
            pltpu.VMEM((total, 1, LANES), jnp.float32),
            dma((local * hidden // block,)),
            dma,
            dma((groups,)),
            dma((groups,)),
            dma((chips,)),
            dma((chips,)),
            dma((chips,)),
            dma((chips,)),
            dma((total,)),
            dma((total,)),
        ],
        compiler_params=pltpu.CompilerParams(
            collective_id=0, has_side_effects=True, vmem_limit_bytes=60 << 20
        ),
        name="gather_project",
    )(payload, gate_pre, up_pre, w_down)

    piece = 512
    small = pl.BlockSpec((1, rows, piece), lambda e, b: (e, 0, b))
    grad_gate_pre, grad_up_pre, grad_down, grad_gates = pl.pallas_call(
        functools.partial(finish, rows),
        grid=(local, hidden // piece),
        out_shape=(
            jax.ShapeDtypeStruct(gate_pre.shape, jnp.bfloat16),
            jax.ShapeDtypeStruct(gate_pre.shape, jnp.bfloat16),
            jax.ShapeDtypeStruct(w_down.shape, jnp.bfloat16),
            jax.ShapeDtypeStruct((tokens, 2), jnp.float32),
        ),
        in_specs=[
            small,
            pl.BlockSpec((1, padded, width), lambda e, b: (e, 0, 0)),
            pl.BlockSpec((1, padded, LANES), lambda e, b: (e, 0, 0)),
            small,
            small,
            pl.BlockSpec((tokens, 2), lambda e, b: (0, 0)),
        ],
        out_specs=(
            small,
            small,
            pl.BlockSpec((1, piece, width), lambda e, b: (e, b, 0)),
            pl.BlockSpec((tokens, 2), lambda e, b: (0, 0)),
        ),
        compiler_params=pltpu.CompilerParams(vmem_limit_bytes=60 << 20),
        name="finish",
    )(proj, rows_in, gates, gate_pre, up_pre, sums)
    return grad_gates, grad_gate_pre, grad_up_pre, grad_down


def per_device(out_grad, routes, gate_values, gate_pre, up_pre, w_down):
    fits = fused_fits(
        lax.axis_size("dp"), lax.axis_size("expert"), *out_grad.shape, *gate_pre.shape
    )
    chosen = fused_device if fits else general_device
    return chosen(out_grad, routes, gate_values, gate_pre, up_pre, w_down)


def solution(mesh):
    return jax.shard_map(
        per_device,
        mesh=mesh,
        in_specs=(
            P(("dp", "expert"), None),
            P("dp", None),
            P(("dp", "expert"), None),
            P("expert", None, "dp"),
            P("expert", None, "dp"),
            P("expert", "dp", None),
        ),
        out_specs=(
            P(("dp", "expert"), None),
            P("expert", None, "dp"),
            P("expert", None, "dp"),
            P("expert", "dp", None),
        ),
        check_vma=False,
    )
```

profile of v0, /device:TPU:0, one launch (start us, length us, event | category | flops | bytes accessed | tf_op | source)
XLA Modules:
  0.0 50.6 jit_solution(12093425214423977116)
XLA Ops:
  0.6 0.8 %copy.16 = s32[8,2]{1,0:T(8,128)S(1)} copy(s32[8,2]{0,1:T(2,128)} %param.7) | data formatting | bytes 128 | tf_op args[1]
  1.4 0.1 eq.27
  1.5 0.1 stack_reshape.3
  1.6 0.2 convert_reduce_fusion
  1.8 0.1 copy.18
  1.9 0.1 reshape.34
  1.9 0.1 select_reduce_fusion
  2.0 0.7 %fusion.3 = bf16[2,128]{1,0:T(2,128)(2,1)S(1)} fusion(bf16[2,2]{1,0:T(2,128)(2,1)} %param.8, bf16[2,4]{1,0:T(2,128)(2,1)S(1)} %convert_element_type.9), kind=kLoop, calls=%fused_computation.10 | loop fusion | flops 1792 | bytes 536 | tf_op jit(solution)/shard_map/concatenate | solution.py:332
  2.8 0.7 %reshape.33 = bf16[16,512]{1,0:T(8,128)(2,1)S(1)} reshape(bf16[2,4096]{1,0:T(2,128)(2,1)} %param.6) | data formatting | bytes 32768 | tf_op jit(solution)/shard_map/reshape | solution.py:335
  3.5 0.6 %pad_maximum_fusion.payload = bf16[16,640]{1,0:T(8,128)(2,1)} fusion(bf16[16,128]{1,0:T(8,128)(2,1)S(1)} %broadcast_bitcast_fusion, bf16[16,512]{1,0:T(8,128)(2,1)S(1)} %reshape.33), kind=kLoop, calls=%fused_computation | loop fusion | flops 40960 | bytes 40960 | tf_op jit(solution)/shard_map/concatenate | solution.py:335
  4.1 33.9 %gather_project.1 = (bf16[2,32,4096]{2,1,0:T(8,128)(2,1)}, f32[2,32,128]{2,1,0:T(8,128)}, f32[2,24,1536]{2,1,0:T(8,128)}, f32[2,2]{1,0:T(2,128)}) custom-call(bf16[16,640]{1,0:T(8,128)(2,1)} %pad_maximum_fusion.payload, bf16[2,24,1536]{2,1,0:T(8,128)(2,1)} %gate_pre.3, bf16[2,24,1536]{2,1,0:T(8,128)(2,1)} %up_pre.3, bf16[2,1536,4096]{2,1,0:T(8,128)(2,1)} %weights.1), custom_call_target="tpu_custom_call" | custom-call | tf_op jit(solution)/shard_map/gather_project/pallas_call | solution.py:340
  38.0 12.6 %finish.1 = (bf16[2,24,1536]{2,1,0:T(8,128)(2,1)}, bf16[2,24,1536]{2,1,0:T(8,128)(2,1)}, bf16[2,1536,4096]{2,1,0:T(8,128)(2,1)}, f32[2,2]{1,0:T(2,128)}) custom-call(f32[2,24,1536]{2,1,0:T(8,128)} %get-tuple-element.12.proj, bf16[2,32,4096]{2,1,0:T(8,128)(2,1)} %get-tuple-element.13.rows_in, f32[2,32,128]{2,1,0:T(8,128)} %get-tuple-element.14.gates, ...), custom_call_target="tpu_custom_call" | custom-call | tf_op jit(solution)/shard_map/finish/pallas_call | solution.py:376
  (5 shorter events, 0.0 us)
where the time goes:
time: 50.9 us; the launch traced here: 50.6 us
  Pallas kernels  46.5 us (91%)
  local copies, waits for them, and re-layouts  1.82 us (4%)
  other arithmetic  1.64 us (3%)
  between operations  0.67 us (1%)
    pallas_call x1, Pallas kernels, fused_device(): pl.pallas_call(functools.partial(gather_project, n_dp, groups, split, loc...  33.9 us
    pallas_call x1, Pallas kernels, fused_device(): pl.pallas_call(functools.partial(finish, rows), grid=(local, hidden // pi...  12.6 us

commit v1 on v0

v1 whole, which is shorter than its diff:
```python
import functools

import jax
import jax.numpy as jnp
from jax import lax
from jax.experimental import pallas as pl
from jax.experimental.pallas import tpu as pltpu
from jax.sharding import PartitionSpec as P

SLOTS = 3


def expert_terms(gate_piece, up_piece, weights, rows_in, gate_row):
    projected = jnp.einsum("erd,efd->erf", rows_in, weights, preferred_element_type=jnp.float32)
    gate_act = gate_piece.astype(jnp.float32)
    up_act = up_piece.astype(jnp.float32)
    sigmoid_val = jax.nn.sigmoid(gate_act)
    silu_val = gate_act * sigmoid_val
    hidden = silu_val * up_act
    partial_value = jnp.sum(hidden * projected, axis=2)
    scale_col = gate_row.astype(jnp.float32)[:, :, None]
    weighted = (scale_col * hidden).astype(jnp.bfloat16)
    down_term = jnp.einsum("erf,erd->efd", weighted, rows_in, preferred_element_type=jnp.float32)
    grad_hidden = scale_col * projected
    grad_gate = (
        grad_hidden * up_act * sigmoid_val * (1.0 + gate_act * (1.0 - sigmoid_val))
    ).astype(jnp.bfloat16)
    grad_up = (grad_hidden * silu_val).astype(jnp.bfloat16)
    return (partial_value, grad_gate, grad_up, down_term)


def general_device(out_grad, routes, gate_values, gate_pre, up_pre, w_down):
    groups = lax.axis_size("expert")
    local_count = gate_pre.shape[0]
    experts = local_count * groups
    tok_count = out_grad.shape[0]
    my_rank = lax.axis_index("expert")
    flat_routes = routes.reshape(-1)
    onehot = (flat_routes[:, None] == jnp.arange(experts, dtype=jnp.int32)[None, :]).astype(
        jnp.int32
    )
    position = jnp.sum((jnp.cumsum(onehot, axis=0) - 1) * onehot, axis=1)
    own_expert = lax.dynamic_slice_in_dim(flat_routes, my_rank * tok_count * 2, tok_count * 2)
    own_position = lax.dynamic_slice_in_dim(position, my_rank * tok_count * 2, tok_count * 2)
    target = own_expert * SLOTS + own_position
    selector = target[:, None] == jnp.arange(experts * SLOTS, dtype=jnp.int32)[None, :]
    picker = selector.astype(jnp.bfloat16).T
    pair_rows = jnp.repeat(out_grad, 2, axis=0)
    send_rows = (
        jnp.dot(picker, pair_rows, preferred_element_type=jnp.float32)
        .astype(jnp.bfloat16)
        .reshape(experts, SLOTS, -1)
    )
    send_gates = (
        jnp.dot(picker, gate_values.reshape(-1, 1), preferred_element_type=jnp.float32)
        .astype(jnp.bfloat16)
        .reshape(experts, SLOTS)
    )
    got_rows, got_gates = (
        lax.all_to_all(send_rows, "expert", split_axis=0, concat_axis=0, tiled=True),
        lax.all_to_all(send_gates, "expert", split_axis=0, concat_axis=0, tiled=True),
    )
    dispatched = jnp.sum(
        got_rows.reshape(groups, local_count, SLOTS, -1).astype(jnp.float32), axis=0
    ).astype(jnp.bfloat16)
    slot_gate = jnp.sum(
        got_gates.reshape(groups, local_count, SLOTS).astype(jnp.float32), axis=0
    ).astype(jnp.bfloat16)
    all_rows, all_gates = (
        lax.all_gather(dispatched, "dp", axis=1, tiled=True),
        lax.all_gather(slot_gate, "dp", axis=1, tiled=True),
    )
    partial_value, grad_gate_pre, grad_up_pre, down_sum = expert_terms(
        gate_pre, up_pre, w_down, all_rows, all_gates
    )
    grad_down = down_sum.astype(jnp.bfloat16)
    own_sums = lax.psum_scatter(partial_value, "dp", scatter_dimension=1, tiled=True)
    score_table = lax.all_gather(own_sums, "expert", axis=0, tiled=True)
    picked = jnp.sum(jnp.where(selector, score_table.reshape(1, -1), 0.0), axis=1)
    grad_gates = picked.reshape(tok_count, 2)
    return (grad_gates, grad_gate_pre, grad_up_pre, grad_down)


LANES = 128
CORES = 2
PAD = 4
MESH = pl.DeviceIdType.MESH
BF16 = jnp.bfloat16
F32 = jnp.float32


def fused_fits(n_dp, groups, tokens, width, local, rows, hidden):
    return (
        n_dp % CORES == 0
        and n_dp > CORES
        and groups > 1
        and local * PAD == 8
        and rows == n_dp * SLOTS
        and n_dp * 8 <= LANES
        and groups * tokens <= LANES
        and width % (4 * LANES) == 0
        and hidden % 512 == 0
        and n_dp * groups <= 64
        and local * hidden * width * 2 <= 26 << 20
    )


def gather_project(
    n_dp, groups, local, rows, block, pieces, early,
    grad, routes, gates, gate_pre, up_pre, weights,
    rows_out, turned_out, grad_gate_out, grad_up_out, sums_out,
    held, tokens_in, gates_in, routes_in, gate_in, up_in,
    table, picked, high, totals, silu_kept, slope_kept, turned_kept,
    sums_own, sums_all,
    load_sem, in_sem, send_z, recv_z, send_g, recv_g, send_c, recv_c, send_p, recv_p,
    send_s, recv_s,
):
    me_dp, me_z = lax.axis_index("dp"), lax.axis_index("expert")
    total = n_dp * groups
    me = me_dp * groups + me_z
    chips = n_dp // CORES
    chip, core = me_dp // CORES, lax.rem(me_dp, CORES)
    partner = chip * CORES + (1 - core)
    tokens, width = grad.shape
    hidden = held.shape[1]
    per = hidden // block
    steps = local * per
    half = width // 2
    full = n_dp * 8
    span = tokens * groups

    barrier = pltpu.get_barrier_semaphore()
    peers = [(me_dp, lax.rem(me_z + dz, groups)) for dz in range(1, groups)]
    peers += [(lax.rem(chip + dc, chips) * CORES + core, me_z) for dc in range(1, chips)]
    peers += [(partner, me_z)]
    for peer in peers:
        pl.semaphore_signal(barrier, inc=1, device_id=peer, device_id_type=MESH)

    def local_copy(src, dst, at):
        copy = pltpu.make_async_copy(src, dst, in_sem.at[at])
        copy.start()
        return copy

    own_rows = local_copy(grad, tokens_in.at[me_z], 0)
    own_gates = local_copy(gates, gates_in.at[me_z], 1)
    own_routes = local_copy(routes, routes_in, 2)
    own_pre = local_copy(gate_pre, gate_in, 3)
    own_up = local_copy(up_pre, up_in, 4)

    def weight_copy(i):
        e, b = i // per, lax.rem(i, per)
        where = pl.ds(b * block, block)
        return pltpu.make_async_copy(weights.at[e, where], held.at[e, where], load_sem.at[i])

    for i in range(steps):
        weight_copy(i).start()

    own_routes.wait()
    first, second = routes_in[0:1, :], routes_in[1:2, :]
    row8 = lax.broadcasted_iota(jnp.int32, (8, 1), 0)
    lane8 = lax.broadcasted_iota(jnp.int32, (1, span), 1)
    expert_of = me_z * local + row8 // PAD
    slot_of = lax.rem(row8, PAD)
    by_choice = [(route == expert_of) for route in (first, second)]
    named = jnp.where(by_choice[0] | by_choice[1], 1, 0)
    before = jnp.zeros((8, span), jnp.int32)
    for t in range(span - 1):
        before = before + jnp.where(lane8 > t, named[:, t : t + 1], 0)
    fills = (before == slot_of) & (named > 0)
    select = jnp.where(fills, 1.0, 0.0)
    select_by = [jnp.where(fills & choice, 1.0, 0.0) for choice in by_choice]

    own_rows.wait()
    own_gates.wait()
    pl.semaphore_wait(barrier, len(peers))
    stage_one = []
    for dz in range(1, groups):
        peer = (me_dp, lax.rem(me_z + dz, groups))
        for ref, s_sem, r_sem in ((tokens_in, send_z, recv_z), (gates_in, send_g, recv_g)):
            copy = pltpu.make_async_remote_copy(
                src_ref=ref.at[me_z], dst_ref=ref.at[me_z],
                send_sem=s_sem.at[dz], recv_sem=r_sem.at[dz],
                device_id=peer, device_id_type=MESH,
            )
            copy.start()
            stage_one.append(copy)

    own_pre.wait()
    own_up.wait()
    wide_row = lax.broadcasted_iota(jnp.int32, (full, 1), 0)
    pair_row = lax.broadcasted_iota(jnp.int32, (1, rows), 1)
    spot = (wide_row // 8) * SLOTS + lax.rem(wide_row, PAD)
    real = lax.rem(wide_row, PAD) < SLOTS
    spread = []
    for e in range(local):
        mine = real & (lax.rem(wide_row, 8) // PAD == e)
        spread.append(jnp.where(mine & (spot == pair_row), 1.0, 0.0))
    flip_row = lax.broadcasted_iota(jnp.int32, (rows, 1), 0)
    flip_col = lax.broadcasted_iota(jnp.int32, (1, full), 1)
    flip_spot = (flip_col // 8) * SLOTS + lax.rem(flip_col, PAD)
    flip_real = lax.rem(flip_col, PAD) < SLOTS
    unspread = []
    for e in range(local):
        mine = flip_real & (lax.rem(flip_col, 8) // PAD == e)
        unspread.append(jnp.where(mine & (flip_spot == flip_row), 1.0, 0.0).astype(BF16))

    owner = lax.rem(wide_row, 8) // PAD
    for c in range(0, hidden, 512):
        cols = slice(c, c + 512)
        gate_act = jnp.zeros((full, 512), F32)
        up_act = jnp.zeros((full, 512), F32)
        for e in range(local):
            pick = spread[e].astype(BF16)
            gate_act += jnp.dot(pick, gate_in[e, :, cols], preferred_element_type=F32)
            up_act += jnp.dot(pick, up_in[e, :, cols], preferred_element_type=F32)
        sigmoid_val = jax.nn.sigmoid(gate_act)
        silu_val = gate_act * sigmoid_val
        act = silu_val * up_act
        silu_kept[:, cols] = silu_val
        slope_kept[:, cols] = up_act * sigmoid_val * (1.0 + gate_act * (1.0 - sigmoid_val))
        turned_kept[cols, :] = act.T
        for e in range(local):
            part = jnp.where(owner == e, act, 0.0)
            top = part.astype(BF16)
            rest = (part - top.astype(F32)).astype(BF16)
            for b in range(512 // block):
                at = slice(b * block, (b + 1) * block)
                high[e * per + c // block + b, :full] = top[:, at]
                high[e * per + c // block + b, full:] = rest[:, at]

    def forward_step(i):
        e, b = i // per, lax.rem(i, per)
        weight_copy(i).wait()
        left = high[i]
        for n in range(0, width, 512):
            totals[:, n : n + 512] += jnp.dot(
                left,
                held[e, pl.ds(pl.multiple_of(b * block, block), block), n : n + 512],
                preferred_element_type=F32,
            )

    def forward_steps(low, top):
        def body(i, carry):
            forward_step(i)
            return carry

        lax.fori_loop(low, top, body, 0)

    totals[...] = jnp.zeros_like(totals)
    forward_steps(0, early[0])

    for copy in stage_one:
        copy.wait_recv()
    slots = jnp.zeros((8, width), F32)
    gate = jnp.zeros((8, 1), F32)
    for z in range(groups):
        got = tokens_in[z].astype(F32)
        got_gate = gates_in[z].astype(F32)
        for t in range(tokens):
            at = z * tokens + t
            slots = slots + select[:, at : at + 1] * got[t : t + 1, :]
            for k in range(2):
                gate = gate + select_by[k][:, at : at + 1] * got_gate[t : t + 1, k : k + 1]
    gate_wide = jnp.broadcast_to(gate, (8, LANES))
    base = pl.multiple_of(me_dp * 16, 16)
    table[pl.ds(base, 16), :half] = jnp.concatenate(
        [slots[:, :half], slots[:, half:]], axis=0
    ).astype(BF16)
    table[pl.ds(base, 16), half:] = jnp.concatenate([gate_wide, gate_wide], axis=0).astype(BF16)

    def block_copy(dp_index, target, piece, s_sem, r_sem):
        where = table.at[pl.ds(dp_index * 16, 16), pl.ds(pieces[piece], pieces[piece + 1] - pieces[piece])]
        copy = pltpu.make_async_remote_copy(
            src_ref=where, dst_ref=where, send_sem=s_sem, recv_sem=r_sem,
            device_id=(target, me_z), device_id_type=MESH,
        )
        copy.start()
        return copy

    count = len(pieces) - 1
    stage_two = {}
    stage_three = {}
    for p in range(count):
        for dc in range(1, chips):
            target = lax.rem(chip + dc, chips) * CORES + core
            stage_two[p, dc] = block_copy(me_dp, target, p, send_c.at[p, dc], recv_c.at[p, dc])
        stage_three[p, 0] = block_copy(me_dp, partner, p, send_p.at[p, 0], recv_p.at[p, 0])

    forward_steps(early[0], early[1])

    for p in range(count):
        for dc in range(1, chips):
            stage_two[p, dc].wait_recv()
            source = lax.rem(chip - dc + chips, chips) * CORES + core
            stage_three[p, dc] = block_copy(source, partner, p, send_p.at[p, dc], recv_p.at[p, dc])

    forward_steps(early[1], steps)

    for copy in stage_three.values():
        copy.wait_recv()

    part = jnp.zeros((full, LANES), F32)
    for h in range(2):
        for n in range(0, half, 512):
            got = table[:, n : n + 512].astype(F32).reshape(n_dp, 16, 512)
            got = got[:, h * 8 : h * 8 + 8].reshape(full, 512)
            at = slice(h * half + n, h * half + n + 512)
            picked[:, at] = got.astype(BF16)
            term = got * (totals[:full, at] + totals[full:, at])
            for q in range(0, 512, LANES):
                part = part + term[:, q : q + LANES]
    rows_out[...] = picked[...]
    part = jnp.sum(part, axis=1, keepdims=True)
    lane = lax.broadcasted_iota(jnp.int32, (full, LANES), 1)
    sums = jnp.sum(jnp.where(lane == wide_row, part, 0.0), axis=0, keepdims=True)
    sums_own[...] = sums
    sums_all[me] = sums
    last = []
    for off in range(1, total):
        other = lax.rem(me + off, total)
        copy = pltpu.make_async_remote_copy(
            src_ref=sums_own, dst_ref=sums_all.at[me],
            send_sem=send_s.at[off], recv_sem=recv_s.at[off],
            device_id=(other // groups, lax.rem(other, groups)), device_id_type=MESH,
        )
        copy.start()
        last.append(copy)

    scale = table[:, half:].astype(F32).reshape(n_dp, 16, LANES)[:, :8].reshape(full, LANES)
    scale_row = scale.T[0:1, :]
    scale_col = scale[:, 0:1]
    col = lax.broadcasted_iota(jnp.int32, (1, full), 1)
    for e in range(local):
        factor = jnp.where(lax.rem(col, 8) // PAD == e, scale_row, 0.0)
        turned_out[e] = (turned_kept[...] * factor).astype(BF16)
    for c in range(0, hidden, 512):
        cols = slice(c, c + 512)
        both = [
            lax.dot_general(
                picked[...], held[e, cols], (((1,), (1,)), ((), ())),
                preferred_element_type=F32,
            )
            for e in range(local)
        ]
        proj = both[0]
        for e in range(1, local):
            proj = jnp.where(owner == e, both[e], proj)
        grad_hidden = scale_col * proj
        gate_grad = (grad_hidden * slope_kept[:, cols]).astype(BF16)
        up_grad = (grad_hidden * silu_kept[:, cols]).astype(BF16)
        for e in range(local):
            for ref, value in ((grad_gate_out, gate_grad), (grad_up_out, up_grad)):
                ref[e, :, cols] = jnp.dot(
                    unspread[e], value, preferred_element_type=F32
                ).astype(BF16)

    for copy in last:
        copy.wait_recv()
    sums_by = []
    for z in range(groups):
        acc = sums_all[z]
        for d in range(1, n_dp):
            acc = acc + sums_all[d * groups + z]
        sums_by.append(acc)
    out_row = lax.broadcasted_iota(jnp.int32, sums_out.shape, 0)
    out_col = lax.broadcasted_iota(jnp.int32, sums_out.shape, 1)
    spots = lax.broadcasted_iota(jnp.int32, (1, LANES), 1)
    result = jnp.zeros(sums_out.shape, F32)
    for k, route in enumerate((first, second)):
        ahead = jnp.zeros((1, span), jnp.int32)
        for t in range(span - 1):
            same = (first[:, t : t + 1] == route) | (second[:, t : t + 1] == route)
            ahead = ahead + jnp.where((lane8 > t) & same, 1, 0)
        for t in range(tokens):
            here = lane8 == me_z * tokens + t
            expert = jnp.sum(jnp.where(here, route, 0), axis=1, keepdims=True)
            place = jnp.sum(jnp.where(here, ahead, 0), axis=1, keepdims=True)
            value = jnp.zeros((1, LANES), F32)
            for z in range(groups):
                offset = expert - z * local
                code = jnp.where(
                    (offset >= 0) & (offset < local), me_dp * 8 + offset * PAD + place, -1
                )
                value = value + jnp.where(spots == code, sums_by[z], 0.0)
            value = jnp.sum(value, axis=1, keepdims=True)
            result = jnp.where((out_row == t) & (out_col == k), value, result)
    sums_out[...] = result
    for copy in stage_one + list(stage_two.values()) + list(stage_three.values()) + last:
        copy.wait_send()


def finish(
    block, rows_in, turned, gate_grad, up_grad, sums,
    grad_sums, grad_gate, grad_up, grad_down, made, small_sem, out_sem,
):
    local, hidden, _ = turned.shape
    width = rows_in.shape[1]
    per = hidden // block
    small = []
    for at, (src, dst) in enumerate(
        ((sums, grad_sums), (gate_grad, grad_gate), (up_grad, grad_up))
    ):
        copy = pltpu.make_async_copy(src, dst, small_sem.at[at])
        copy.start()
        small.append(copy)

    def out_copy(i):
        e, b = i // per, lax.rem(i, per)
        where = pl.ds(b * block, block)
        return pltpu.make_async_copy(made.at[e, where], grad_down.at[e, where], out_sem.at[i])

    def body(i, carry):
        e, b = i // per, lax.rem(i, per)
        where = pl.ds(pl.multiple_of(b * block, block), block)
        left = turned[e, where, :]
        for n in range(0, width, 512):
            made[e, where, n : n + 512] = jnp.dot(
                left, rows_in[:, n : n + 512], preferred_element_type=F32
            ).astype(BF16)
        out_copy(i).start()
        return carry

    lax.fori_loop(0, local * per, body, 0)

    def drain(i, carry):
        out_copy(i).wait()
        return carry

    lax.fori_loop(0, local * per, drain, 0)
    for copy in small:
        copy.wait()


def fused_device(out_grad, routes, gate_values, gate_pre, up_pre, w_down):
    n_dp, groups = lax.axis_size("dp"), lax.axis_size("expert")
    tokens, width = out_grad.shape
    local, rows, hidden = gate_pre.shape
    block = 512
    total = n_dp * groups
    full = n_dp * 8
    half = width // 2
    chips = n_dp // CORES
    pieces = (0, half // 2, half + LANES)
    count = len(pieces) - 1
    steps = local * hidden // block
    early = (steps // 2, steps - 1)
    span = groups * tokens

    vmem = pl.BlockSpec(memory_space=pltpu.VMEM)
    hbm = pl.BlockSpec(memory_space=pltpu.HBM)
    dma = pltpu.SemaphoreType.DMA
    scratch = pltpu.VMEM
    rows_in, turned, gate_grad, up_grad, sums = pl.pallas_call(
        functools.partial(gather_project, n_dp, groups, local, rows, block, pieces, early),
        out_shape=(
            pltpu.VMEM((full, width), BF16),
            pltpu.VMEM((local, hidden, full), BF16),
            pltpu.VMEM(gate_pre.shape, BF16),
            pltpu.VMEM(up_pre.shape, BF16),
            pltpu.VMEM((tokens, 2), F32),
        ),
        in_specs=[hbm] * 6,
        out_specs=(vmem,) * 5,
        scratch_shapes=[
            scratch((local, hidden, width), BF16),
            scratch((groups, tokens, width), BF16),
            scratch((groups, tokens, 2), BF16),
            scratch((2, span), jnp.int32),
            scratch(gate_pre.shape, BF16),
            scratch(up_pre.shape, BF16),
            scratch((n_dp * 16, half + LANES), BF16),
            scratch((full, width), BF16),
            scratch((steps, 2 * full, block), BF16),
            scratch((2 * full, width), F32),
            scratch((full, hidden), F32),
            scratch((full, hidden), F32),
            scratch((hidden, full), F32),
            scratch((1, LANES), F32),
            scratch((total, 1, LANES), F32),
            dma((steps,)),
            dma((5,)),
            dma((groups,)),
            dma((groups,)),
            dma((groups,)),
            dma((groups,)),
            dma((count, chips)),
            dma((count, chips)),
            dma((count, chips)),
            dma((count, chips)),
            dma((total,)),
            dma((total,)),
        ],
        compiler_params=pltpu.CompilerParams(
            collective_id=0, has_side_effects=True, vmem_limit_bytes=52 << 20
        ),
        name="gather_project",
    )(out_grad, routes.T, gate_values, gate_pre, up_pre, w_down)

    piece = 256
    return pl.pallas_call(
        functools.partial(finish, piece),
        out_shape=(
            jax.ShapeDtypeStruct((tokens, 2), F32),
            jax.ShapeDtypeStruct(gate_pre.shape, BF16),
            jax.ShapeDtypeStruct(up_pre.shape, BF16),
            jax.ShapeDtypeStruct(w_down.shape, BF16),
        ),
        in_specs=[vmem] * 5,
        out_specs=(hbm,) * 4,
        scratch_shapes=[
            scratch((local, hidden, width), BF16),
            dma((3,)),
            dma((local * hidden // piece,)),
        ],
        compiler_params=pltpu.CompilerParams(vmem_limit_bytes=52 << 20),
        name="finish",
    )(rows_in, turned, gate_grad, up_grad, sums)


def per_device(out_grad, routes, gate_values, gate_pre, up_pre, w_down):
    fits = fused_fits(
        lax.axis_size("dp"), lax.axis_size("expert"), *out_grad.shape, *gate_pre.shape
    )
    chosen = fused_device if fits else general_device
    return chosen(out_grad, routes, gate_values, gate_pre, up_pre, w_down)


def solution(mesh):
    return jax.shard_map(
        per_device,
        mesh=mesh,
        in_specs=(
            P(("dp", "expert"), None),
            P("dp", None),
            P(("dp", "expert"), None),
            P("expert", None, "dp"),
            P("expert", None, "dp"),
            P("expert", "dp", None),
        ),
        out_specs=(
            P(("dp", "expert"), None),
            P("expert", None, "dp"),
            P("expert", None, "dp"),
            P("expert", "dp", None),
        ),
        check_vma=False,
    )
```

time: 50.9 us -> 39.5 us (0.78)
  Pallas kernels: 46.5 us -> 34.7 us
  local copies, waits for them, and re-layouts: 1.82 us -> 3.86 us
  other arithmetic: 1.64 us -> 0 us
    pallas_call x2, Pallas kernels: 46.5 us -> 34.7 us  [the longest x1 24.9 us: fused_device(): pl.pallas_call(functools.partial(gather_project, n_dp, groups, local, row...]
    unnamed x1 -> x10, local copies, waits for them, and re-layouts: 0.76 us -> 3.86 us
    concatenate x2 -> x0, other arithmetic: 1.35 us -> none  [the longest x1 0.74 us: fused_device(): meta = jnp.concatenate([codes, gate_values], axis=1)]
    reshape x3 -> x0, local copies, waits for them, and re-layouts: 0.82 us -> none  [the longest x1 0.73 us: fused_device(): payload = jnp.concatenate([out_grad.reshape(16, chunk), meta], axis=1)]
where the time goes in v1:
time: 39.5 us; the launch traced here: 39.2 us
  Pallas kernels  34.7 us (88%)
  local copies, waits for them, and re-layouts  3.86 us (10%)
  between operations  0.65 us (2%)
    pallas_call x1, Pallas kernels, fused_device(): pl.pallas_call(functools.partial(gather_project, n_dp, groups, local, row...  24.9 us
    pallas_call x1, Pallas kernels, fused_device(): pl.pallas_call(functools.partial(finish, piece), out_shape=(jax.ShapeDtyp...  9.75 us
    unnamed x10, local copies, waits for them, and re-layouts  3.86 us

profile of v1, /device:TPU:0, one launch (start us, length us, event | category | flops | bytes accessed | tf_op | source)
XLA Modules:
  0.0 39.2 jit_solution(6726790000411393586)
XLA Ops:
  0.6 0.0 copy-start
  0.6 0.9 %copy-done = bf16[2,24,1536]{2,1,0:T(8,128)(2,1)S(1)} copy-done((bf16[2,24,1536]{2,1,0:T(8,128)(2,1)S(1)}, bf16[2,24,1536]{2,1,0:T(8,128)(2,1)}, u32[]{:S(2)}) %copy-start) | copy-done | bytes 147480
  1.5 0.0 copy-start.1
  1.5 0.9 %copy-done.1 = bf16[2,24,1536]{2,1,0:T(8,128)(2,1)S(1)} copy-done((bf16[2,24,1536]{2,1,0:T(8,128)(2,1)S(1)}, bf16[2,24,1536]{2,1,0:T(8,128)(2,1)}, u32[]{:S(2)}) %copy-start.1) | copy-done | bytes 147480
  2.5 0.0 copy-start.2
  2.5 0.7 %copy-done.2 = bf16[2,4096]{1,0:T(2,128)(2,1)S(1)} copy-done((bf16[2,4096]{1,0:T(2,128)(2,1)S(1)}, bf16[2,4096]{1,0:T(2,128)(2,1)}, u32[]{:S(2)}) %copy-start.2) | copy-done | bytes 16408
  3.2 0.0 copy-start.3
  3.2 0.7 %copy-done.3 = s32[8,2]{0,1:T(2,128)S(1)} copy-done((s32[8,2]{0,1:T(2,128)S(1)}, s32[8,2]{0,1:T(2,128)}, u32[]{:S(2)}) %copy-start.3) | copy-done | bytes 88
  3.9 0.0 copy-start.4
  3.9 0.7 %copy-done.4 = bf16[2,2]{1,0:T(2,128)(2,1)S(1)} copy-done((bf16[2,2]{1,0:T(2,128)(2,1)S(1)}, bf16[2,2]{1,0:T(2,128)(2,1)}, u32[]{:S(2)}) %copy-start.4) | copy-done | bytes 32
  4.5 24.9 %gather_project.1 = (bf16[64,4096]{1,0:T(8,128)(2,1)S(1)}, bf16[2,1536,64]{2,1,0:T(8,128)(2,1)S(1)}, bf16[2,24,1536]{2,1,0:T(8,128)(2,1)S(1)}, bf16[2,24,1536]{2,1,0:T(8,128)(2,1)S(1)}, f32[2,2]{1,0:T(2,128)S(1)}) custom-call(bf16[2,4096]{1,0:T(2,128)(2,1)S(1)} %copy-done.2, s32[2,8]{1,0:T(2,128)S(1)} %bitcast.1, bf16[2,2]{1,0:T(2,128)(2,1)S(1)} %copy-done.4, ...), custom_call_target="tpu_custom_call" | custom-call | tf_op jit(solution)/shard_map/gather_project/pallas_call | solution.py:453
  29.4 9.8 %finish.1 = (f32[2,2]{1,0:T(2,128)}, bf16[2,24,1536]{2,1,0:T(8,128)(2,1)}, bf16[2,24,1536]{2,1,0:T(8,128)(2,1)}, bf16[2,1536,4096]{2,1,0:T(8,128)(2,1)}) custom-call(bf16[64,4096]{1,0:T(8,128)(2,1)S(1)} %get-tuple-element.9.rows_in, bf16[2,1536,64]{2,1,0:T(8,128)(2,1)S(1)} %get-tuple-element.10.turned, bf16[2,24,1536]{2,1,0:T(8,128)(2,1)S(1)} %get-tuple-element.11.gate_grad, ...), custom_call_target="tpu_custom_call" | custom-call | tf_op jit(solution)/shard_map/finish/pallas_call | solution.py:500
Async XLA Ops:
  0.6 0.9 %copy-start = (bf16[2,24,1536]{2,1,0:T(8,128)(2,1)S(1)}, bf16[2,24,1536]{2,1,0:T(8,128)(2,1)}, u32[]{:S(2)}) copy-start(bf16[2,24,1536]{2,1,0:T(8,128)(2,1)} %gate_pre.1) | copy-start | bytes 442372
  1.5 0.9 %copy-start.1 = (bf16[2,24,1536]{2,1,0:T(8,128)(2,1)S(1)}, bf16[2,24,1536]{2,1,0:T(8,128)(2,1)}, u32[]{:S(2)}) copy-start(bf16[2,24,1536]{2,1,0:T(8,128)(2,1)} %up_pre.1) | copy-start | bytes 442372
  2.5 0.7 %copy-start.2 = (bf16[2,4096]{1,0:T(2,128)(2,1)S(1)}, bf16[2,4096]{1,0:T(2,128)(2,1)}, u32[]{:S(2)}) copy-start(bf16[2,4096]{1,0:T(2,128)(2,1)} %grad.1) | copy-start | bytes 49156
  3.2 0.7 %copy-start.3 = (s32[8,2]{0,1:T(2,128)S(1)}, s32[8,2]{0,1:T(2,128)}, u32[]{:S(2)}) copy-start(s32[8,2]{0,1:T(2,128)} %param.7) | copy-start | bytes 196
  3.9 0.7 %copy-start.4 = (bf16[2,2]{1,0:T(2,128)(2,1)S(1)}, bf16[2,2]{1,0:T(2,128)(2,1)}, u32[]{:S(2)}) copy-start(bf16[2,2]{1,0:T(2,128)(2,1)} %gates.1) | copy-start | bytes 28

commit v2 on v1

--- a/solution.py
+++ b/solution.py
@@ -106,11 +106,11 @@
 
 
 def gather_project(
-    n_dp, groups, local, rows, block, pieces, early,
+    n_dp, groups, local, rows, block, pieces, early, flipped,
     grad, routes, gates, gate_pre, up_pre, weights,
     rows_out, turned_out, grad_gate_out, grad_up_out, sums_out,
     held, tokens_in, gates_in, routes_in, gate_in, up_in,
-    table, picked, high, totals, silu_kept, slope_kept, turned_kept,
+    table, picked, high, totals, flips, silu_kept, slope_kept, turned_kept,
     sums_own, sums_all,
     load_sem, in_sem, send_z, recv_z, send_g, recv_g, send_c, recv_c, send_p, recv_p,
     send_s, recv_s,
@@ -152,9 +152,6 @@
         where = pl.ds(b * block, block)
         return pltpu.make_async_copy(weights.at[e, where], held.at[e, where], load_sem.at[i])
 
-    for i in range(steps):
-        weight_copy(i).start()
-
     own_routes.wait()
     first, second = routes_in[0:1, :], routes_in[1:2, :]
     row8 = lax.broadcasted_iota(jnp.int32, (8, 1), 0)
@@ -172,6 +169,11 @@
 
     own_rows.wait()
     own_gates.wait()
+    own_pre.wait()
+    own_up.wait()
+    for i in range(steps):
+        weight_copy(i).start()
+
     pl.semaphore_wait(barrier, len(peers))
     stage_one = []
     for dz in range(1, groups):
@@ -185,8 +187,6 @@
             copy.start()
             stage_one.append(copy)
 
-    own_pre.wait()
-    own_up.wait()
     wide_row = lax.broadcasted_iota(jnp.int32, (full, 1), 0)
     pair_row = lax.broadcasted_iota(jnp.int32, (1, rows), 1)
     spot = (wide_row // 8) * SLOTS + lax.rem(wide_row, PAD)
@@ -228,23 +228,26 @@
                 high[e * per + c // block + b, :full] = top[:, at]
                 high[e * per + c // block + b, full:] = rest[:, at]
 
-    def forward_step(i):
+    def forward_step(i, flip):
         e, b = i // per, lax.rem(i, per)
         weight_copy(i).wait()
         left = high[i]
         for n in range(0, width, 512):
-            totals[:, n : n + 512] += jnp.dot(
-                left,
-                held[e, pl.ds(pl.multiple_of(b * block, block), block), n : n + 512],
-                preferred_element_type=F32,
-            )
+            right = held[e, pl.ds(pl.multiple_of(b * block, block), block), n : n + 512]
+            totals[:, n : n + 512] += jnp.dot(left, right, preferred_element_type=F32)
+            if flip:
+                flips[i, n : n + 512, :] = right.T
 
     def forward_steps(low, top):
-        def body(i, carry):
-            forward_step(i)
+        def body(flip, i, carry):
+            forward_step(i, flip)
             return carry
 
-        lax.fori_loop(low, top, body, 0)
+        middle = min(max(low, flipped), top)
+        if middle > low:
+            lax.fori_loop(low, middle, functools.partial(body, True), 0)
+        if top > middle:
+            lax.fori_loop(middle, top, functools.partial(body, False), 0)
 
     totals[...] = jnp.zeros_like(totals)
     forward_steps(0, early[0])
@@ -335,13 +338,18 @@
         turned_out[e] = (turned_kept[...] * factor).astype(BF16)
     for c in range(0, hidden, 512):
         cols = slice(c, c + 512)
-        both = [
-            lax.dot_general(
-                picked[...], held[e, cols], (((1,), (1,)), ((), ())),
-                preferred_element_type=F32,
-            )
-            for e in range(local)
-        ]
+        both = []
+        for e in range(local):
+            i = e * per + c // block
+            if i < flipped:
+                both.append(jnp.dot(picked[...], flips[i], preferred_element_type=F32))
+            else:
+                both.append(
+                    lax.dot_general(
+                        picked[...], held[e, cols], (((1,), (1,)), ((), ())),
+                        preferred_element_type=F32,
+                    )
+                )
         proj = both[0]
         for e in range(1, local):
             proj = jnp.where(owner == e, both[e], proj)
@@ -420,7 +428,7 @@
         out_copy(i).start()
         return carry
 
-    lax.fori_loop(0, local * per, body, 0)
+    lax.fori_loop(0, local * per, body, 0, unroll=2)
 
     def drain(i, carry):
         out_copy(i).wait()
@@ -440,18 +448,23 @@
     full = n_dp * 8
     half = width // 2
     chips = n_dp // CORES
-    pieces = (0, half // 2, half + LANES)
+    pieces = (0, half + LANES)
     count = len(pieces) - 1
     steps = local * hidden // block
-    early = (steps // 2, steps - 1)
+    early = (steps // 3, steps - 1)
+    flipped = steps
     span = groups * tokens
 
     vmem = pl.BlockSpec(memory_space=pltpu.VMEM)
     hbm = pl.BlockSpec(memory_space=pltpu.HBM)
     dma = pltpu.SemaphoreType.DMA
     scratch = pltpu.VMEM
+    placed = [
+        pltpu.with_memory_space_constraint(ref, pltpu.HBM)
+        for ref in (out_grad, routes.T, gate_values, gate_pre, up_pre, w_down)
+    ]
     rows_in, turned, gate_grad, up_grad, sums = pl.pallas_call(
-        functools.partial(gather_project, n_dp, groups, local, rows, block, pieces, early),
+        functools.partial(gather_project, n_dp, groups, local, rows, block, pieces, early, flipped),
         out_shape=(
             pltpu.VMEM((full, width), BF16),
             pltpu.VMEM((local, hidden, full), BF16),
@@ -472,6 +485,7 @@
             scratch((full, width), BF16),
             scratch((steps, 2 * full, block), BF16),
             scratch((2 * full, width), F32),
+            scratch((flipped, width, block), BF16),
             scratch((full, hidden), F32),
             scratch((full, hidden), F32),
             scratch((hidden, full), F32),
@@ -491,10 +505,10 @@
             dma((total,)),
         ],
         compiler_params=pltpu.CompilerParams(
-            collective_id=0, has_side_effects=True, vmem_limit_bytes=52 << 20
+            collective_id=0, has_side_effects=True, vmem_limit_bytes=59 << 20
         ),
         name="gather_project",
-    )(out_grad, routes.T, gate_values, gate_pre, up_pre, w_down)
+    )(*placed)
 
     piece = 256
     return pl.pallas_call(

time: 39.5 us -> 31.9 us (0.81)
  local copies, waits for them, and re-layouts: 3.86 us -> 0 us
  Pallas kernels: 34.7 us -> 31.1 us
    unnamed x10 -> x0, local copies, waits for them, and re-layouts: 3.86 us -> none
    pallas_call x1, Pallas kernels: 24.9 us -> 21.9 us  [fused_device(): pl.pallas_call(functools.partial(gather_project, n_dp, groups, local, row...]
    pallas_call x1, Pallas kernels: 9.75 us -> 9.2 us  [fused_device(): pl.pallas_call(functools.partial(finish, piece), out_shape=(jax.ShapeDtyp...]
where the time goes in v2:
time: 31.9 us; the launch traced here: 31.7 us
  Pallas kernels  31.1 us (97%)
  between operations  0.64 us (2%)
    pallas_call x1, Pallas kernels, fused_device(): pl.pallas_call(functools.partial(gather_project, n_dp, groups, local, row...  21.9 us
    pallas_call x1, Pallas kernels, fused_device(): pl.pallas_call(functools.partial(finish, piece), out_shape=(jax.ShapeDtyp...  9.2 us

profile of v2, /device:TPU:0, one launch (start us, length us, event | category | flops | bytes accessed | tf_op | source)
XLA Modules:
  0.0 31.7 jit_solution(653934644542275225)
XLA Ops:
  0.6 21.9 %gather_project.1 = (bf16[64,4096]{1,0:T(8,128)(2,1)S(1)}, bf16[2,1536,64]{2,1,0:T(8,128)(2,1)S(1)}, bf16[2,24,1536]{2,1,0:T(8,128)(2,1)S(1)}, bf16[2,24,1536]{2,1,0:T(8,128)(2,1)S(1)}, f32[2,2]{1,0:T(2,128)S(1)}) custom-call(bf16[2,4096]{1,0:T(2,128)(2,1)} %grad.1, s32[2,8]{1,0:T(2,128)} %bitcast.1, bf16[2,2]{1,0:T(2,128)(2,1)} %gates.1, ...), custom_call_target="tpu_custom_call" | custom-call | tf_op jit(solution)/shard_map/gather_project/pallas_call | solution.py:466
  22.5 9.2 %finish.1 = (f32[2,2]{1,0:T(2,128)}, bf16[2,24,1536]{2,1,0:T(8,128)(2,1)}, bf16[2,24,1536]{2,1,0:T(8,128)(2,1)}, bf16[2,1536,4096]{2,1,0:T(8,128)(2,1)}) custom-call(bf16[64,4096]{1,0:T(8,128)(2,1)S(1)} %get-tuple-element.9.rows_in, bf16[2,1536,64]{2,1,0:T(8,128)(2,1)S(1)} %get-tuple-element.10.turned, bf16[2,24,1536]{2,1,0:T(8,128)(2,1)S(1)} %get-tuple-element.11.gate_grad, ...), custom_call_target="tpu_custom_call" | custom-call | tf_op jit(solution)/shard_map/finish/pallas_call | solution.py:514

commit v3 on v2

--- a/solution.py
+++ b/solution.py
@@ -89,11 +89,21 @@
 F32 = jnp.float32
 
 
+def pow2(n):
+    return n & (n - 1) == 0
+
+
+def far_first(n):
+    return sorted(range(1, n), reverse=True)
+
+
 def fused_fits(n_dp, groups, tokens, width, local, rows, hidden):
     return (
         n_dp % CORES == 0
         and n_dp > CORES
         and groups > 1
+        and pow2(groups)
+        and pow2(n_dp)
         and local * PAD == 8
         and rows == n_dp * SLOTS
         and n_dp * 8 <= LANES
@@ -110,7 +120,7 @@
     grad, routes, gates, gate_pre, up_pre, weights,
     rows_out, turned_out, grad_gate_out, grad_up_out, sums_out,
     held, tokens_in, gates_in, routes_in, gate_in, up_in,
-    table, picked, high, totals, flips, silu_kept, slope_kept, turned_kept,
+    table, high, totals, flips, silu_kept, slope_kept, turned_kept,
     sums_own, sums_all,
     load_sem, in_sem, send_z, recv_z, send_g, recv_g, send_c, recv_c, send_p, recv_p,
     send_s, recv_s,
@@ -130,8 +140,8 @@
     span = tokens * groups
 
     barrier = pltpu.get_barrier_semaphore()
-    peers = [(me_dp, lax.rem(me_z + dz, groups)) for dz in range(1, groups)]
-    peers += [(lax.rem(chip + dc, chips) * CORES + core, me_z) for dc in range(1, chips)]
+    peers = [(me_dp, me_z ^ dz) for dz in far_first(groups)]
+    peers += [((chip ^ dc) * CORES + core, me_z) for dc in far_first(chips)]
     peers += [(partner, me_z)]
     for peer in peers:
         pl.semaphore_signal(barrier, inc=1, device_id=peer, device_id_type=MESH)
@@ -169,15 +179,16 @@
 
     own_rows.wait()
     own_gates.wait()
+    weight_copy(0).start()
     own_pre.wait()
     own_up.wait()
-    for i in range(steps):
+    for i in range(1, steps):
         weight_copy(i).start()
 
     pl.semaphore_wait(barrier, len(peers))
     stage_one = []
-    for dz in range(1, groups):
-        peer = (me_dp, lax.rem(me_z + dz, groups))
+    for dz in far_first(groups):
+        peer = (me_dp, me_z ^ dz)
         for ref, s_sem, r_sem in ((tokens_in, send_z, recv_z), (gates_in, send_g, recv_g)):
             copy = pltpu.make_async_remote_copy(
                 src_ref=ref.at[me_z], dst_ref=ref.at[me_z],
@@ -228,6 +239,11 @@
                 high[e * per + c // block + b, :full] = top[:, at]
                 high[e * per + c // block + b, full:] = rest[:, at]
 
+    eye_row = lax.broadcasted_iota(jnp.int32, (256, 256), 0)
+    eye_col = lax.broadcasted_iota(jnp.int32, (256, 256), 1)
+    eye = jnp.where(eye_row == eye_col, 1.0, 0.0).astype(BF16)
+    by_product = (width // 1024,)
+
     def forward_step(i, flip):
         e, b = i // per, lax.rem(i, per)
         weight_copy(i).wait()
@@ -235,7 +251,13 @@
         for n in range(0, width, 512):
             right = held[e, pl.ds(pl.multiple_of(b * block, block), block), n : n + 512]
             totals[:, n : n + 512] += jnp.dot(left, right, preferred_element_type=F32)
-            if flip:
+            if flip and n // 512 in by_product:
+                for q in range(0, 512, 256):
+                    flips[i, n + q : n + q + 256, :] = lax.dot_general(
+                        eye, right[:, q : q + 256], (((1,), (1,)), ((), ())),
+                        preferred_element_type=F32,
+                    ).astype(BF16)
+            elif flip:
                 flips[i, n : n + 512, :] = right.T
 
     def forward_steps(low, top):
@@ -284,8 +306,8 @@
     stage_two = {}
     stage_three = {}
     for p in range(count):
-        for dc in range(1, chips):
-            target = lax.rem(chip + dc, chips) * CORES + core
+        for dc in far_first(chips):
+            target = (chip ^ dc) * CORES + core
             stage_two[p, dc] = block_copy(me_dp, target, p, send_c.at[p, dc], recv_c.at[p, dc])
         stage_three[p, 0] = block_copy(me_dp, partner, p, send_p.at[p, 0], recv_p.at[p, 0])
 
@@ -294,10 +316,13 @@
     for p in range(count):
         for dc in range(1, chips):
             stage_two[p, dc].wait_recv()
-            source = lax.rem(chip - dc + chips, chips) * CORES + core
+            source = (chip ^ dc) * CORES + core
             stage_three[p, dc] = block_copy(source, partner, p, send_p.at[p, dc], recv_p.at[p, dc])
 
     forward_steps(early[1], steps)
+
+    for n in range(0, width, 512):
+        totals[:full, n : n + 512] += totals[full:, n : n + 512]
 
     for copy in stage_three.values():
         copy.wait_recv()
@@ -308,23 +333,22 @@
             got = table[:, n : n + 512].astype(F32).reshape(n_dp, 16, 512)
             got = got[:, h * 8 : h * 8 + 8].reshape(full, 512)
             at = slice(h * half + n, h * half + n + 512)
-            picked[:, at] = got.astype(BF16)
-            term = got * (totals[:full, at] + totals[full:, at])
+            rows_out[:, at] = got.astype(BF16)
+            term = got * totals[:full, at]
             for q in range(0, 512, LANES):
                 part = part + term[:, q : q + LANES]
-    rows_out[...] = picked[...]
     part = jnp.sum(part, axis=1, keepdims=True)
     lane = lax.broadcasted_iota(jnp.int32, (full, LANES), 1)
     sums = jnp.sum(jnp.where(lane == wide_row, part, 0.0), axis=0, keepdims=True)
     sums_own[...] = sums
     sums_all[me] = sums
     last = []
-    for off in range(1, total):
-        other = lax.rem(me + off, total)
+    offsets = [(dp, z) for z in range(groups) for dp in range(n_dp)][1:]
+    for off, (dp, z) in sorted(enumerate(offsets, 1), reverse=True):
         copy = pltpu.make_async_remote_copy(
             src_ref=sums_own, dst_ref=sums_all.at[me],
             send_sem=send_s.at[off], recv_sem=recv_s.at[off],
-            device_id=(other // groups, lax.rem(other, groups)), device_id_type=MESH,
+            device_id=(me_dp ^ dp, me_z ^ z), device_id_type=MESH,
         )
         copy.start()
         last.append(copy)
@@ -342,11 +366,11 @@
         for e in range(local):
             i = e * per + c // block
             if i < flipped:
-                both.append(jnp.dot(picked[...], flips[i], preferred_element_type=F32))
+                both.append(jnp.dot(rows_out[...], flips[i], preferred_element_type=F32))
             else:
                 both.append(
                     lax.dot_general(
-                        picked[...], held[e, cols], (((1,), (1,)), ((), ())),
+                        rows_out[...], held[e, cols], (((1,), (1,)), ((), ())),
                         preferred_element_type=F32,
                     )
                 )
@@ -362,18 +386,10 @@
                     unspread[e], value, preferred_element_type=F32
                 ).astype(BF16)
 
-    for copy in last:
-        copy.wait_recv()
-    sums_by = []
-    for z in range(groups):
-        acc = sums_all[z]
-        for d in range(1, n_dp):
-            acc = acc + sums_all[d * groups + z]
-        sums_by.append(acc)
     out_row = lax.broadcasted_iota(jnp.int32, sums_out.shape, 0)
     out_col = lax.broadcasted_iota(jnp.int32, sums_out.shape, 1)
     spots = lax.broadcasted_iota(jnp.int32, (1, LANES), 1)
-    result = jnp.zeros(sums_out.shape, F32)
+    masks = {}
     for k, route in enumerate((first, second)):
         ahead = jnp.zeros((1, span), jnp.int32)
         for t in range(span - 1):
@@ -383,13 +399,26 @@
             here = lane8 == me_z * tokens + t
             expert = jnp.sum(jnp.where(here, route, 0), axis=1, keepdims=True)
             place = jnp.sum(jnp.where(here, ahead, 0), axis=1, keepdims=True)
-            value = jnp.zeros((1, LANES), F32)
             for z in range(groups):
                 offset = expert - z * local
                 code = jnp.where(
                     (offset >= 0) & (offset < local), me_dp * 8 + offset * PAD + place, -1
                 )
-                value = value + jnp.where(spots == code, sums_by[z], 0.0)
+                masks[t, k, z] = jnp.where(spots == code, 1.0, 0.0)
+    for copy in last:
+        copy.wait_recv()
+    sums_by = []
+    for z in range(groups):
+        acc = sums_all[z]
+        for d in range(1, n_dp):
+            acc = acc + sums_all[d * groups + z]
+        sums_by.append(acc)
+    result = jnp.zeros(sums_out.shape, F32)
+    for t in range(tokens):
+        for k in range(2):
+            value = jnp.zeros((1, LANES), F32)
+            for z in range(groups):
+                value = value + jnp.where(masks[t, k, z] > 0.5, sums_by[z], 0.0)
             value = jnp.sum(value, axis=1, keepdims=True)
             result = jnp.where((out_row == t) & (out_col == k), value, result)
     sums_out[...] = result
@@ -417,25 +446,38 @@
         where = pl.ds(b * block, block)
         return pltpu.make_async_copy(made.at[e, where], grad_down.at[e, where], out_sem.at[i])
 
-    def body(i, carry):
-        e, b = i // per, lax.rem(i, per)
-        where = pl.ds(pl.multiple_of(b * block, block), block)
+    def make(e, where):
         left = turned[e, where, :]
         for n in range(0, width, 512):
             made[e, where, n : n + 512] = jnp.dot(
                 left, rows_in[:, n : n + 512], preferred_element_type=F32
             ).astype(BF16)
+
+    def body(i, carry):
+        e, b = i // per, lax.rem(i, per)
+        make(e, pl.ds(pl.multiple_of(b * block, block), block))
         out_copy(i).start()
         return carry
 
-    lax.fori_loop(0, local * per, body, 0, unroll=2)
+    part = block // 2
+    first = []
+    for q in range(2):
+        where = pl.ds(q * part, part)
+        make(0, where)
+        copy = pltpu.make_async_copy(
+            made.at[0, where], grad_down.at[0, where], small_sem.at[3 + q]
+        )
+        copy.start()
+        first.append(copy)
+    body(1, 0)
+    lax.fori_loop(2, local * per, body, 0, unroll=2)
 
     def drain(i, carry):
         out_copy(i).wait()
         return carry
 
-    lax.fori_loop(0, local * per, drain, 0)
-    for copy in small:
+    lax.fori_loop(1, local * per, drain, 0)
+    for copy in small + first:
         copy.wait()
 
 
@@ -482,7 +524,6 @@
             scratch(gate_pre.shape, BF16),
             scratch(up_pre.shape, BF16),
             scratch((n_dp * 16, half + LANES), BF16),
-            scratch((full, width), BF16),
             scratch((steps, 2 * full, block), BF16),
             scratch((2 * full, width), F32),
             scratch((flipped, width, block), BF16),
@@ -523,7 +564,7 @@
         out_specs=(hbm,) * 4,
         scratch_shapes=[
             scratch((local, hidden, width), BF16),
-            dma((3,)),
+            dma((5,)),
             dma((local * hidden // piece,)),
         ],
         compiler_params=pltpu.CompilerParams(vmem_limit_bytes=52 << 20),

time: 31.9 us -> 31.3 us (0.981)
  Pallas kernels: 31.1 us -> 30.5 us
    pallas_call x1, Pallas kernels: 21.9 us -> 21.4 us  [fused_device(): pl.pallas_call(functools.partial(gather_project, n_dp, groups, local, row...]
where the time goes in v3:
time: 31.3 us; the launch traced here: 31.1 us
  Pallas kernels  30.5 us (97%)
  between operations  0.64 us (2%)
    pallas_call x1, Pallas kernels, fused_device(): pl.pallas_call(functools.partial(gather_project, n_dp, groups, local, row...  21.4 us
    pallas_call x1, Pallas kernels, fused_device(): pl.pallas_call(functools.partial(finish, piece), out_shape=(jax.ShapeDtyp...  9.08 us

profile of v3, /device:TPU:0, one launch (start us, length us, event | category | flops | bytes accessed | tf_op | source)
XLA Modules:
  0.0 31.1 jit_solution(2652620334327989336)
XLA Ops:
  0.6 21.4 %gather_project.1 = (bf16[64,4096]{1,0:T(8,128)(2,1)S(1)}, bf16[2,1536,64]{2,1,0:T(8,128)(2,1)S(1)}, bf16[2,24,1536]{2,1,0:T(8,128)(2,1)S(1)}, bf16[2,24,1536]{2,1,0:T(8,128)(2,1)S(1)}, f32[2,2]{1,0:T(2,128)S(1)}) custom-call(bf16[2,4096]{1,0:T(2,128)(2,1)} %grad.1, s32[2,8]{1,0:T(2,128)} %bitcast.1, bf16[2,2]{1,0:T(2,128)(2,1)} %gates.1, ...), custom_call_target="tpu_custom_call" | custom-call | tf_op jit(solution)/shard_map/gather_project/pallas_call | solution.py:508
  22.0 9.1 %finish.1 = (f32[2,2]{1,0:T(2,128)}, bf16[2,24,1536]{2,1,0:T(8,128)(2,1)}, bf16[2,24,1536]{2,1,0:T(8,128)(2,1)}, bf16[2,1536,4096]{2,1,0:T(8,128)(2,1)}) custom-call(bf16[64,4096]{1,0:T(8,128)(2,1)S(1)} %get-tuple-element.9.rows_in, bf16[2,1536,64]{2,1,0:T(8,128)(2,1)S(1)} %get-tuple-element.10.turned, bf16[2,24,1536]{2,1,0:T(8,128)(2,1)S(1)} %get-tuple-element.11.gate_grad, ...), custom_call_target="tpu_custom_call" | custom-call | tf_op jit(solution)/shard_map/finish/pallas_call | solution.py:555

commit v4 on v3

--- a/solution.py
+++ b/solution.py
@@ -360,20 +360,17 @@
     for e in range(local):
         factor = jnp.where(lax.rem(col, 8) // PAD == e, scale_row, 0.0)
         turned_out[e] = (turned_kept[...] * factor).astype(BF16)
+    for i in range(flipped, steps):
+        e, b = divmod(i, per)
+        for n in range(0, width, 512):
+            flips[i, n : n + 512, :] = held[e, b * block : (b + 1) * block, n : n + 512].T
     for c in range(0, hidden, 512):
         cols = slice(c, c + 512)
         both = []
         for e in range(local):
-            i = e * per + c // block
-            if i < flipped:
-                both.append(jnp.dot(rows_out[...], flips[i], preferred_element_type=F32))
-            else:
-                both.append(
-                    lax.dot_general(
-                        rows_out[...], held[e, cols], (((1,), (1,)), ((), ())),
-                        preferred_element_type=F32,
-                    )
-                )
+            both.append(
+                jnp.dot(rows_out[...], flips[e * per + c // block], preferred_element_type=F32)
+            )
         proj = both[0]
         for e in range(1, local):
             proj = jnp.where(owner == e, both[e], proj)
@@ -494,7 +491,7 @@
     count = len(pieces) - 1
     steps = local * hidden // block
     early = (steps // 3, steps - 1)
-    flipped = steps
+    flipped = steps - 3
     span = groups * tokens
 
     vmem = pl.BlockSpec(memory_space=pltpu.VMEM)
@@ -526,7 +523,7 @@
             scratch((n_dp * 16, half + LANES), BF16),
             scratch((steps, 2 * full, block), BF16),
             scratch((2 * full, width), F32),
-            scratch((flipped, width, block), BF16),
+            scratch((steps, width, block), BF16),
             scratch((full, hidden), F32),
             scratch((full, hidden), F32),
             scratch((hidden, full), F32),

time: 31.3 us -> 30.8 us (0.984)
  Pallas kernels: 30.5 us -> 30 us
    pallas_call x1, Pallas kernels: 21.4 us -> 20.9 us  [fused_device(): pl.pallas_call(functools.partial(gather_project, n_dp, groups, local, row...]
where the time goes in v4:
time: 30.8 us; the launch traced here: 30.6 us
  Pallas kernels  30 us (97%)
  between operations  0.64 us (2%)
    pallas_call x1, Pallas kernels, fused_device(): pl.pallas_call(functools.partial(gather_project, n_dp, groups, local, row...  20.9 us
    pallas_call x1, Pallas kernels, fused_device(): pl.pallas_call(functools.partial(finish, piece), out_shape=(jax.ShapeDtyp...  9.07 us

profile of v4, /device:TPU:0, one launch (start us, length us, event | category | flops | bytes accessed | tf_op | source)
XLA Modules:
  0.0 30.6 jit_solution(17914388671538091320)
XLA Ops:
  0.6 20.9 %gather_project.1 = (bf16[64,4096]{1,0:T(8,128)(2,1)S(1)}, bf16[2,1536,64]{2,1,0:T(8,128)(2,1)S(1)}, bf16[2,24,1536]{2,1,0:T(8,128)(2,1)S(1)}, bf16[2,24,1536]{2,1,0:T(8,128)(2,1)S(1)}, f32[2,2]{1,0:T(2,128)S(1)}) custom-call(bf16[2,4096]{1,0:T(2,128)(2,1)} %grad.1, s32[2,8]{1,0:T(2,128)} %bitcast.1, bf16[2,2]{1,0:T(2,128)(2,1)} %gates.1, ...), custom_call_target="tpu_custom_call" | custom-call | tf_op jit(solution)/shard_map/gather_project/pallas_call | solution.py:505
  21.6 9.1 %finish.1 = (f32[2,2]{1,0:T(2,128)}, bf16[2,24,1536]{2,1,0:T(8,128)(2,1)}, bf16[2,24,1536]{2,1,0:T(8,128)(2,1)}, bf16[2,1536,4096]{2,1,0:T(8,128)(2,1)}) custom-call(bf16[64,4096]{1,0:T(8,128)(2,1)S(1)} %get-tuple-element.9.rows_in, bf16[2,1536,64]{2,1,0:T(8,128)(2,1)S(1)} %get-tuple-element.10.turned, bf16[2,24,1536]{2,1,0:T(8,128)(2,1)S(1)} %get-tuple-element.11.gate_grad, ...), custom_call_target="tpu_custom_call" | custom-call | tf_op jit(solution)/shard_map/finish/pallas_call | solution.py:552
